TPU v7x, 256 devices: a 8x8x2 block of a 8x8x16 slice. The times are simulated.
256 devices in a mesh: groups: 2 (over z), seq: 16 (over y, core), dp: 8 (over x).
Axes of the slice: x: 8, y: 8, z: 2, core: 2. Of those that a mesh axis runs over, the one named last changes fastest.
The devices are a block of a 8x8x16 slice.
Arguments:
- resid: bfloat16 [16, 1024, 2048], P(('groups', 'dp'), 'seq'), parts along dimension 0, may hold values from -6 to 6
- queries_keys: bfloat16 [2, 16, 1024, 2048], P(None, ('groups', 'dp'), 'seq'), parts along dimension 1, may hold values from -20 to 20
- values: bfloat16 [16, 1024, 2048], P(('groups', 'dp'), 'seq'), parts along dimension 0, may hold values from -6 to 6
- doc_ids: int32 [16, 1024], P(('groups', 'dp')), parts along dimension 0, may hold values from 0 to 5, never falling along the last dimension, each value on 1 to 512 neighbouring positions
- out_weight: bfloat16 [2048, 2048], P(None, 'dp'), may hold values from -0.125 to 0.125
- norm_gain: float32 [2048], replicated, may hold values from 0.5 to 1.5
- expert_ids: int32 [16, 1024, 4], P(('groups', 'dp'), 'seq'), parts along dimension 0, may hold values from 0 to 31, all different within a row; in each aligned block of 64 rows (0 to 63, 64 to 127, ..., all dimensions but the last counted through in order) at most 10 rows name the same one
- gate_vals: float32 [16, 1024, 4], P(('groups', 'dp'), 'seq'), parts along dimension 0, may hold values from 0.05 to 0.6
- expert_gate: bfloat16 [128, 2048, 352], P(('seq', 'dp')), may hold values from -0.125 to 0.125
- expert_up: bfloat16 [128, 2048, 352], P(('seq', 'dp')), may hold values from -0.125 to 0.125
- expert_down: bfloat16 [128, 352, 2048], P(('seq', 'dp')), may hold values from -0.15625 to 0.15625
- shared_gate: bfloat16 [2048, 2816], P(None, 'dp'), may hold values from -0.125 to 0.125
- shared_up: bfloat16 [2048, 2816], P(None, 'dp'), may hold values from -0.125 to 0.125
- shared_down: bfloat16 [2816, 2048], P('dp'), may hold values from -0.109375 to 0.109375
- shared_score: bfloat16 [2048], replicated, may hold values from -0.125 to 0.125
Outputs:
- layer_out: bfloat16 [16, 1024, 2048], P(('groups', 'dp'), 'seq'), parts along dimension 0
There are 2 independent parts, one for each index of `groups`. A program takes and returns all parts, laid end to end along the dimension named above; an argument that names none is the same for every part. Nothing has to cross between parts.
Inputs may be any that keep to these rules, and one draw needn't show every extreme that they name: `doc_ids`: document numbers never fall along a sequence; each document holds 1 to 512 positions. `expert_ids`: each token names 4 different experts; among the rows of one device no expert is named more than 10 times.
All inputs are finite; a program needn't handle non-finite values.
Results may differ from a plain program's by a relative error of at most 0.01.
Values may be sent and summed in bfloat16 or wider, within the bound.
A program may use at most 128 MiB of HBM per device.

v0:
```python
import functools
import math

import jax
import jax.numpy as jnp
from jax import lax
from jax.experimental import pallas as pl
from jax.experimental.pallas import tpu as pltpu
from jax.sharding import PartitionSpec as P

HD = 128
TOPK = 4
SPLIT = 4
CAP = 10
GROUP = 2
CORES = 2

norm_eps = 1e-06
MESH = pl.DeviceIdType.MESH
F32 = jnp.float32
BF16 = jnp.bfloat16


def ring_delta(j):
    return ((j + 1) // 2) * (2 * (j % 2) - 1)


class Ring:
    def __init__(self, nd, axis, source, place, send_sem, recv_sem):
        self.nd, self.axis, self.last = nd, axis, nd // 2
        self.source, self.place = source, place
        self.send_sem, self.recv_sem = send_sem, recv_sem
        self.me = lax.axis_index(axis)

    def behind(self, t, way):
        return lax.rem(self.me - (1 - 2 * way) * t + self.nd, self.nd)

    def hop(self, way, t, sub):
        index = self.behind(t - 1, way)
        src = self.source(sub) if t == 1 else self.place(index, sub)
        return pltpu.make_async_remote_copy(
            src, self.place(index, sub), self.send_sem.at[way, t - 1, sub],
            self.recv_sem.at[way, t - 1, sub],
            device_id={self.axis: self.behind(-1, way)}, device_id_type=MESH,
        )

    def hops(self, t):
        return [
            (way, t, sub)
            for sub in range(2)
            for way in range(2)
            if t < self.last or (t == self.last and sub == way)
        ]

    def start(self):
        for h in self.hops(1):
            self.hop(*h).start()

    def advance(self, t):
        following = self.hops(t + 1)
        for way, _, sub in self.hops(t):
            self.hop(way, t, sub).wait_recv()
            if (way, t + 1, sub) in following:
                self.hop(way, t + 1, sub).start()

    def arrived(self, t):
        return [self.behind(t, 0), self.behind(t, 1)] if t < self.last else [self.behind(t, 0)]

    def finish(self):
        for t in range(1, self.last + 1):
            for h in self.hops(t):
                self.hop(*h).wait_send()


def greet(axes):
    barrier = pltpu.get_barrier_semaphore()
    for axis, size in axes.items():
        me = lax.axis_index(axis)

        @pl.loop(1, size)
        def _(k):
            pl.semaphore_signal(
                barrier, inc=1, device_id={axis: lax.rem(me + k, size)}, device_id_type=MESH
            )

    pl.semaphore_wait(barrier, sum(axes.values()) - len(axes))


def layer_kernel(
    ns, nd, docs_ref, info_ref, vecs_ref, qk_hbm, v_hbm, resid_hbm, w_hbm, eg_hbm, eu_hbm, ed_hbm,
    sg_hbm, su_hbm, sd_hbm, out_ref,
    qk, v, resid, wg, wu, wd, vg, vu, vd, dcol, info, routes, qh, kh, vh, att, mixed, wall, own_sum,
    send_sum, got_sum, residual, normed, every, picks, mixes, send, own_in, pair_in, act, pair_out,
    pair_part, own_part, back, ret, total, landed, passed,
    w_sem, local_sem, si_sem, ri_sem, so_sem, ro_sem, sd_sem, rd_sem, sp_sem, rp_sem, sw_sem, rw_sem,
    sg_sem, rg_sem, sy_sem, ry_sem, sx_sem, rx_sem, sq_sem, rq_sem, sr_sem, rr_sem, s2_sem, r2_sem,
):
    s = lax.axis_index("seq")
    d = lax.axis_index("dp")
    rows, width = v.shape
    length = rows * ns
    tokens = rows * nd
    core = lax.rem(s, CORES)
    chips = ns // CORES
    depth = width // CORES
    block = width // nd
    chip_rows = rows * CORES
    half = width // 2
    quarter = half // 2
    lanes = 2 * rows

    first = [
        pltpu.make_async_copy(src, dst, w_sem.at[i])
        for i, (src, dst) in enumerate(
            (
                (qk_hbm, qk), (v_hbm, v),
                (w_hbm.at[pl.ds(pl.multiple_of(core * depth, 16), depth)], wall.at[d]),
                (resid_hbm, resid),
            )
        )
    ]
    later = [
        pltpu.make_async_copy(src, dst, w_sem.at[4 + i])
        for i, (src, dst) in enumerate(
            (
                (sg_hbm, vg), (su_hbm, vu), (sd_hbm, vd),
                (eg_hbm.at[0], wg), (eu_hbm.at[0], wu), (ed_hbm.at[0], wd),
            )
        )
    ]
    for c in first:
        c.start()

    experts = ns * nd // SPLIT
    lane = lax.broadcasted_iota(jnp.int32, (1, lanes), 1)
    valid = (lane >= lax.rem(d, 2) * rows) & (lane < (lax.rem(d, 2) + 1) * rows)
    expert = lax.broadcasted_iota(jnp.int32, (experts, lanes), 0).astype(F32)
    chosen_ids = [jnp.where(valid, info_ref[k : k + 1, :], -1.0) for k in range(TOPK)]
    named = [ids == expert for ids in chosen_ids]
    earlier = lax.broadcasted_iota(jnp.int32, (lanes, lanes), 0) < lax.broadcasted_iota(
        jnp.int32, (lanes, lanes), 1
    )
    counts = jnp.dot(
        jnp.where(functools.reduce(jnp.logical_or, named), 1.0, 0.0).astype(BF16),
        jnp.where(earlier, 1.0, 0.0).astype(BF16),
        preferred_element_type=F32,
    )
    for k in range(TOPK):
        rank = jnp.sum(jnp.where(named[k], counts, 0.0), axis=0, keepdims=True)
        info[k : k + 1, :] = jnp.where(valid, chosen_ids[k] * CAP + rank, 0.0)
    info[TOPK:, :] = info_ref[TOPK:, :]
    routes[d] = info[...]
    docs = docs_ref[...].astype(F32)
    for i in range(length // HD):
        tile = jnp.broadcast_to(docs[:, i * HD : (i + 1) * HD], (HD, HD))
        dcol[i * HD : (i + 1) * HD, :] = tile.T

    greet({"seq": ns, "dp": nd})
    first[0].wait()
    first[1].wait()

    def own_rows(ref, t):
        return ref.at[pl.ds(pl.multiple_of(t * rows, 16), rows)]

    def cols(t):
        return pl.ds(pl.multiple_of(t * HD, HD), HD)

    def info_copy(to, slot):
        return pltpu.make_async_remote_copy(
            info, routes.at[slot], sd_sem.at[to], rd_sem.at[slot],
            device_id={"dp": to}, device_id_type=MESH,
        )

    def pieces(t):
        return (
            (qk.at[0, :, cols(t)], qh),
            (qk.at[1, :, cols(t)], kh),
            (v.at[:, cols(t)], vh),
        )

    def in_copies(j, to, slot):
        return [
            pltpu.make_async_remote_copy(
                src, own_rows(dst, slot), si_sem.at[c, j], ri_sem.at[c, j],
                device_id={"seq": to}, device_id_type=MESH,
            )
            for c, (src, dst) in enumerate(pieces(to))
        ]

    def toward(j):
        return lax.rem(s - ring_delta(j) + ns, ns)

    def origin(j):
        return lax.rem(s + ring_delta(j) + ns, ns)

    @pl.loop(1, ns)
    def _(j):
        for c in in_copies(j, toward(j), s):
            c.start()

    w_part = depth // 2
    weights = Ring(
        nd, "dp",
        lambda sub: wall.at[d, pl.ds(sub * w_part, w_part)],
        lambda index, sub: wall.at[index, pl.ds(sub * w_part, w_part)],
        sw_sem, rw_sem,
    )
    first[2].wait()
    weights.start()

    @pl.loop(1, nd)
    def _(k):
        info_copy(lax.rem(d + k, nd), d).start()

    for c in later:
        c.start()
    local = [
        pltpu.make_async_copy(src, own_rows(dst, s), local_sem.at[c])
        for c, (src, dst) in enumerate(pieces(s))
    ]
    for c in local:
        c.start()
    for c in local:
        c.wait()

    def receive(j):
        frm = origin(j)
        for c in in_copies(j, frm, frm):
            c.wait_recv()

    @pl.loop(1, ns // 2)
    def _(j):
        receive(j)

    weights.advance(1)

    @pl.loop(ns // 2, ns)
    def _(j):
        receive(j)

    per_core = ns // CORES
    mate = s + 1 - 2 * core

    def owner(chip):
        return chip * CORES + s // per_core

    def out_copy(chip, head):
        return pltpu.make_async_remote_copy(
            att.at[pl.ds(pl.multiple_of(chip * chip_rows, 16), chip_rows)],
            mixed.at[:, cols(lax.rem(head, per_core))], so_sem.at[chip],
            ro_sem.at[lax.rem(head, per_core)],
            device_id={"seq": owner(chip)}, device_id_type=MESH,
        )

    scale = 1.0 / math.sqrt(HD)
    step_rows = 2 * chip_rows
    for i in range(length // step_rows):
        upto = (i + 1) * step_rows
        span = pl.ds(i * step_rows, step_rows)
        scores = lax.dot_general(
            qh[span, :], kh[0:upto, :], (((1,), (1,)), ((), ())), preferred_element_type=F32
        ) * scale
        at = lax.broadcasted_iota(jnp.int32, (step_rows, upto), 0) + i * step_rows
        key_at = lax.broadcasted_iota(jnp.int32, (step_rows, upto), 1)
        mine = jnp.concatenate([dcol[span, :]] * (upto // HD), axis=1)
        allowed = (key_at <= at) & (mine == docs[:, 0:upto])
        scores = jnp.where(allowed, scores, -1e30)
        lifted = jnp.exp(scores - jnp.max(scores, axis=-1, keepdims=True))
        probs = (lifted / jnp.sum(lifted, axis=-1, keepdims=True)).astype(BF16)
        att[span, :] = jnp.dot(probs, vh[0:upto, :], preferred_element_type=F32).astype(BF16)
        for chip in (2 * i, 2 * i + 1):

            @pl.when(owner(chip) != s)
            def _():
                out_copy(chip, s).start()

            @pl.when(owner(chip) == s)
            def _():
                mixed[:, cols(lax.rem(s, per_core))] = att[
                    pl.ds(chip * chip_rows, chip_rows), :
                ]

        if i == 1:
            weights.advance(2)

    slots = nd * CAP
    per_seq = nd // SPLIT
    first_expert = d // SPLIT

    @pl.loop(1, nd)
    def _(k):
        other = lax.rem(d + k, nd)
        info_copy(other, other).wait_send()
        info_copy(other, other).wait_recv()

    tiles = [routes[2 * m] + routes[2 * m + 1] for m in range(nd // 2)]
    code = jnp.concatenate([tile[:TOPK] for tile in tiles], axis=1)
    gates = jnp.concatenate([tile[TOPK:] for tile in tiles], axis=1)
    slot = lax.broadcasted_iota(jnp.int32, (slots, tokens), 0).astype(F32)
    token = lax.broadcasted_iota(jnp.int32, (slots, tokens), 1).astype(F32)
    slot_block = jnp.floor((slot + 0.5) * (1.0 / CAP))
    token_block = jnp.floor((token + 0.5) * (1.0 / rows))
    ranks = jnp.where(slot_block == token_block, slot - slot_block * CAP, -1e6)

    def seat(j):
        return pl.ds(pl.multiple_of(j * slots, 16), slots)

    @pl.loop(0, ns)
    def _(j):
        base = ((toward(j) * per_seq + first_expert) * CAP).astype(F32)
        hits = [code[k : k + 1, :] - base == ranks for k in range(TOPK)]
        hit = functools.reduce(jnp.logical_or, hits)
        picks[seat(j), :] = jnp.where(hit, 1.0, 0.0).astype(BF16)
        mixes[seat(j), :] = functools.reduce(
            jnp.add, [jnp.where(hits[k], gates[k : k + 1, :], 0.0) for k in range(TOPK)]
        ).astype(BF16)

    weights.advance(3)

    @pl.loop(0, per_core)
    def _(h):
        @pl.when(core * per_core + h != s)
        def _():
            out_copy(0, h).wait_recv()

    def sum_copy(index):
        at = pl.ds(pl.multiple_of(index * block, block), block)
        return pltpu.make_async_remote_copy(
            send_sum.at[:, at], got_sum.at[:, at], sp_sem.at[index], rp_sem.at[index],
            device_id={"seq": mate}, device_id_type=MESH,
        )

    def project(index):
        at = pl.ds(pl.multiple_of(index * block, block), block)
        theirs = mixed[pl.ds(pl.multiple_of((1 - core) * rows, 16), rows), :]
        mine = mixed[pl.ds(pl.multiple_of(core * rows, 16), rows), :]
        send_sum[:, at] = jnp.dot(theirs, wall[index], preferred_element_type=F32)
        own_sum[:, at] = jnp.dot(mine, wall[index], preferred_element_type=F32)
        sum_copy(index).start()

    project(d)
    for t in range(1, nd // 2 + 1):
        if t >= 4:
            weights.advance(t)
        for index in weights.arrived(t):
            project(index)

    @pl.loop(0, nd)
    def _(index):
        sum_copy(index).wait_recv()

    first[3].wait()
    projected = (own_sum[...] + got_sum[...]).astype(BF16)
    summed = (resid[...].astype(F32) + projected.astype(F32)).astype(BF16)
    residual[...] = summed
    stream = summed.astype(F32)
    scaled = (
        stream
        * lax.rsqrt(jnp.mean(stream * stream, axis=-1, keepdims=True) + norm_eps)
        * vecs_ref[0:1, :]
    ).astype(BF16)

    def place_of(chunk, side):
        return side * half + chunk * quarter

    mine_at = pl.ds(pl.multiple_of(d * rows, 16), rows)
    for chunk in range(2):
        for side in range(2):
            at = place_of(chunk, side)
            normed[chunk, side] = scaled[:, at : at + quarter]
            every[chunk, side, mine_at, :] = scaled[:, at : at + quarter]
    part = rows // 2

    def gather(chunk):
        return Ring(
            nd, "dp",
            lambda sub: normed.at[chunk, :, pl.ds(sub * part, part)],
            lambda index, sub: every.at[
                chunk, :, pl.ds(pl.multiple_of(index * rows + sub * part, 16), part)
            ],
            sg_sem.at[chunk], rg_sem.at[chunk],
        )

    rings = [gather(0), gather(1)]

    par = lax.rem(d, 2)
    partner = d + 1 - 2 * par
    group_slots = GROUP * slots
    groups = ns // GROUP

    def span_of(g):
        return pl.ds(pl.multiple_of(g * group_slots, 16), group_slots)

    def go_copy(chunk, j):
        return pltpu.make_async_remote_copy(
            send.at[chunk, seat(j)], own_in.at[chunk, seat(j)], sy_sem.at[chunk, j],
            ry_sem.at[chunk, j], device_id={"seq": toward(j)}, device_id_type=MESH,
        )

    def swap_copy(chunk, g):
        return pltpu.make_async_remote_copy(
            own_in.at[chunk, span_of(g)], pair_in.at[chunk, span_of(g)], sx_sem.at[chunk, g],
            rx_sem.at[chunk, g], device_id={"dp": partner}, device_id_type=MESH,
        )

    def part_copy(chunk, g):
        return pltpu.make_async_remote_copy(
            pair_out.at[chunk, span_of(g)], pair_part.at[chunk, span_of(g)], sq_sem.at[chunk, g],
            rq_sem.at[chunk, g], device_id={"dp": partner}, device_id_type=MESH,
        )

    def back_copy(chunk, j):
        return pltpu.make_async_remote_copy(
            back.at[chunk, seat(j)], ret.at[chunk, seat(j)], sr_sem.at[chunk, j],
            rr_sem.at[chunk, j], device_id={"seq": origin(j)}, device_id_type=MESH,
        )

    def columns(chunk, side):
        return pl.ds(pl.multiple_of(side * half + chunk * quarter, quarter), quarter)

    batch = ns // 4

    def pick(chunk, q):
        at = pl.ds(q * batch * slots, batch * slots)
        got = jnp.dot(
            picks[at, :], every[chunk, par], preferred_element_type=F32
        ).astype(BF16)
        send[chunk, at, :] = got
        if q == 0:
            own_in[chunk, 0:slots, :] = got[0:slots]

    def go(chunk, q):
        @pl.loop(max(1, q * batch), (q + 1) * batch)
        def _(j):
            go_copy(chunk, j).start()

    rings[0].start()
    rings[0].advance(1)
    rings[0].advance(2)
    rings[1].start()
    rings[0].advance(3)
    rings[0].advance(4)
    for q in range(4):
        pick(0, q)
        if q:
            go(0, q - 1)
        rings[1].advance(q + 1)
    go(0, 3)
    for q in range(4):
        pick(1, q)
        if q:
            go(1, q - 1)
    go(1, 3)
    for c in later:
        c.wait()

    def nt(a, w):
        return lax.dot_general(a, w, (((1,), (1,)), ((), ())), preferred_element_type=F32)

    def silu(a):
        return a / (1.0 + jnp.exp(-a))

    def arrive(chunk, g):
        for i in range(GROUP):
            j = g * GROUP + i

            @pl.when(j > 0)
            def _():
                go_copy(chunk, j).wait_recv()

        swap_copy(chunk, g).start()

    quads = [(chunk, side) for chunk in range(2) for side in range(2)]
    share = tokens // 4

    @pl.loop(0, groups)
    def _(g):
        arrive(0, g)

        @pl.when((g >= 1) & (g <= 4))
        def _():
            at = pl.ds(pl.multiple_of((g - 1) * share, share), share)
            gate_act = jnp.zeros((share, vg.shape[0]), F32)
            up_act = jnp.zeros((share, vg.shape[0]), F32)
            weight = jnp.zeros((share, 1), F32)
            for chunk, side in quads:
                a = every[chunk, side, at, :]
                where = pl.ds(place_of(chunk, side), quarter)
                gate_act += nt(a, vg[:, where])
                up_act += nt(a, vu[:, where])
                weight += jnp.sum(
                    a.astype(F32) * vecs_ref[1:2, where], axis=-1, keepdims=True
                )
            hidden = (silu(gate_act) * up_act).astype(BF16)
            weight = 1.0 / (1.0 + jnp.exp(-weight))
            for chunk, side in quads:
                total[chunk, side, at, :] = weight * jnp.dot(
                    hidden, vd[:, pl.ds(place_of(chunk, side), quarter)],
                    preferred_element_type=F32,
                )

    def down(chunk, g):
        hidden = act[span_of(g), :]
        pair_out[chunk, span_of(g), :] = jnp.dot(
            hidden, wd[:, columns(chunk, 1 - par)], preferred_element_type=F32
        ).astype(BF16)
        own_part[span_of(g), :] = jnp.dot(
            hidden, wd[:, columns(chunk, par)], preferred_element_type=F32
        )
        part_copy(chunk, g).start()

    def join(chunk, g):
        part_copy(chunk, g).wait_recv()
        back[chunk, span_of(g), :] = (
            own_part[span_of(g), :] + pair_part[chunk, span_of(g), :].astype(F32)
        ).astype(BF16)

    def leave(chunk, g):
        for i in range(GROUP):
            j = g * GROUP + i

            @pl.when(j > 0)
            def _():
                back_copy(chunk, j).start()

            @pl.when(j == 0)
            def _():
                ret[chunk, 0:slots, :] = back[chunk, 0:slots, :]

    def combine(chunk, g):
        for i in range(GROUP):
            j = g * GROUP + i

            @pl.when(j > 0)
            def _():
                back_copy(chunk, j).wait_recv()

        total[chunk, par] += lax.dot_general(
            mixes[span_of(g), :], ret[chunk, span_of(g), :], (((0,), (0,)), ((), ())),
            preferred_element_type=F32,
        )

    @pl.loop(0, groups + 2)
    def _(step):
        @pl.when(step < groups)
        def _():
            arrive(1, step)

        @pl.when(step >= 2)
        def _():
            join(0, step - 2)

        @pl.when((step >= 1) & (step <= groups))
        def _():
            g = step - 1
            gate_act = jnp.zeros((group_slots, wg.shape[0]), F32)
            up_act = jnp.zeros((group_slots, wg.shape[0]), F32)
            for chunk in range(2):
                swap_copy(chunk, g).wait_recv()
                for rows_in, side in ((own_in, par), (pair_in, 1 - par)):
                    a = rows_in[chunk, span_of(g), :]
                    gate_act += nt(a, wg[:, columns(chunk, side)])
                    up_act += nt(a, wu[:, columns(chunk, side)])
            act[span_of(g), :] = (silu(gate_act) * up_act).astype(BF16)
            down(0, g)

        @pl.when(step >= 2)
        def _():
            leave(0, step - 2)

    @pl.loop(0, groups)
    def _(g):
        down(1, g)

    @pl.loop(0, groups)
    def _(g):
        join(1, g)
        combine(0, g)
        leave(1, g)

    last = nd // 2

    def own(index, sub):
        return pl.ds(pl.multiple_of(index * rows + sub * part, 16), part)

    def used(way, t, sub):
        return t < last or (t == last and sub == way)

    def hop(chunk, way, t, sub):
        sign = 1 - 2 * way
        return pltpu.make_async_remote_copy(
            passed.at[chunk, way, t - 1, sub], landed.at[chunk, way, t - 1, sub],
            s2_sem.at[chunk, way, t - 1, sub], r2_sem.at[chunk, way, t - 1, sub],
            device_id={"dp": lax.rem(d + sign + nd, nd)}, device_id_type=MESH,
        )

    def target(way, t):
        return lax.rem(d + (1 - 2 * way) * t + nd, nd)

    def reduce_chunk(chunk):
        for t in range(last, 0, -1):
            for sub in range(2):
                for way in range(2):
                    if not used(way, t, sub):
                        continue
                    term = total[chunk, :, own(target(way, t), sub), :]
                    if used(way, t + 1, sub):
                        hop(chunk, way, t + 1, sub).wait_recv()
                        term = term + landed[chunk, way, t, sub].astype(F32)
                    passed[chunk, way, t - 1, sub] = term.astype(BF16)
                    hop(chunk, way, t, sub).start()

    def settle(chunk):
        for sub in range(2):
            for way in range(2):
                hop(chunk, way, 1, sub).wait_recv()
            at = pl.ds(sub * part, part)
            sums = (
                total[chunk, :, own(d, sub), :]
                + landed[chunk, 0, 0, sub].astype(F32)
                + landed[chunk, 1, 0, sub].astype(F32)
            )
            for side in range(2):
                where = pl.ds(place_of(chunk, side), quarter)
                out_ref[at, where] = residual[at, where].astype(F32) + sums[side]

    reduce_chunk(0)

    @pl.loop(0, groups)
    def _(g):
        combine(1, g)

    reduce_chunk(1)
    settle(0)
    settle(1)

    for chunk in range(2):
        for way in range(2):
            for sub in range(2):
                for t in range(1, last + 1):
                    if used(way, t, sub):
                        hop(chunk, way, t, sub).wait_send()
        rings[chunk].finish()

        @pl.loop(1, ns)
        def _(j):
            go_copy(chunk, j).wait_send()
            back_copy(chunk, j).wait_send()

        @pl.loop(0, groups)
        def _(g):
            swap_copy(chunk, g).wait_send()
            part_copy(chunk, g).wait_send()

    weights.finish()

    @pl.loop(1, ns)
    def _(j):
        for c in in_copies(j, toward(j), s):
            c.wait_send()

    @pl.loop(0, chips)
    def _(chip):
        @pl.when(owner(chip) != s)
        def _():
            out_copy(chip, s).wait_send()

    @pl.loop(0, nd)
    def _(index):
        sum_copy(index).wait_send()


def run_layer(docs, info, vecs, qk, v, resid, out_weight, expert_weights, shared_weights, ns, nd):
    rows, width = v.shape
    length = rows * ns
    tokens = rows * nd
    half = width // 2
    quarter = half // 2
    slots = ns * nd * CAP
    groups = ns // GROUP
    hidden = expert_weights[0].shape[1]
    shared_hidden = shared_weights[0].shape[0]
    dma = pltpu.SemaphoreType.DMA
    vmem = pl.BlockSpec(memory_space=pltpu.VMEM)
    anyspace = pl.BlockSpec(memory_space=pl.ANY)

    def buf(*shape):
        return pltpu.VMEM(shape, BF16)

    def wide(*shape):
        return pltpu.VMEM(shape, F32)

    ring = dma((2, nd // 2, 2))
    rings = dma((2, 2, nd // 2, 2))
    per_seat = dma((2, ns))
    per_group = dma((2, groups))
    return pl.pallas_call(
        functools.partial(layer_kernel, ns, nd),
        out_shape=jax.ShapeDtypeStruct((rows, width), F32),
        in_specs=[vmem] * 3 + [anyspace] * 10,
        out_specs=vmem,
        scratch_shapes=[buf(2, rows, width), buf(rows, width), buf(rows, width)]
        + [buf(hidden, width)] * 3
        + [buf(shared_hidden, width)] * 3
        + [wide(length, HD), wide(*info.shape), wide(nd, *info.shape)]
        + [buf(length, HD)] * 4
        + [
            buf(rows * CORES, width // CORES),
            buf(nd, width // CORES, out_weight.shape[1]),
            wide(rows, width), wide(rows, width), wide(rows, width),
            buf(rows, width),
            buf(2, 2, rows, quarter),
            buf(2, 2, tokens, quarter),
            buf(slots, tokens), buf(slots, tokens),
            buf(2, slots, quarter), buf(2, slots, quarter), buf(2, slots, quarter),
            buf(slots, hidden),
            buf(2, slots, quarter), buf(2, slots, quarter),
            wide(slots, quarter),
            buf(2, slots, quarter), buf(2, slots, quarter),
            wide(2, 2, tokens, quarter),
            buf(2, 2, nd // 2, 2, 2, rows // 2, quarter),
            buf(2, 2, nd // 2, 2, 2, rows // 2, quarter),
            dma((10,)), dma((3,)), dma((3, ns)), dma((3, ns)), dma((ns // CORES,)),
            dma((ns // CORES,)), dma((nd,)), dma((nd,)), dma((nd,)), dma((nd,)),
            ring, ring, rings, rings,
            per_seat, per_seat, per_group, per_group, per_group, per_group, per_seat, per_seat,
            rings, rings,
        ],
        compiler_params=pltpu.CompilerParams(
            collective_id=1, has_side_effects=True, vmem_limit_bytes=67043328
        ),
        cost_estimate=pl.CostEstimate(
            flops=12 * slots * half * hidden, bytes_accessed=8 * slots * half, transcendentals=0
        ),
        name="layer",
    )(docs, info, vecs, qk, v, resid, out_weight, *expert_weights, *shared_weights)


def body(
    resid,
    queries_keys,
    values,
    doc_ids,
    out_weight,
    norm_gain,
    expert_ids,
    gate_vals,
    expert_gate,
    expert_up,
    expert_down,
    shared_gate,
    shared_up,
    shared_down,
    shared_score,
):
    ns = lax.axis_size("seq")
    nd = lax.axis_size("dp")
    tokens = resid.shape[1]
    width = resid.shape[2]
    d = lax.axis_index("dp")
    info = jnp.concatenate([expert_ids[0].T.astype(F32), gate_vals[0].T], axis=0)
    blank = jnp.zeros_like(info)
    info = jnp.where(
        d % 2 == 0,
        jnp.concatenate([info, blank], axis=1),
        jnp.concatenate([blank, info], axis=1),
    )
    out = run_layer(
        doc_ids,
        info,
        jnp.stack([norm_gain, shared_score.astype(F32)]),
        queries_keys.reshape(2, tokens, width),
        values[0],
        resid[0],
        out_weight,
        (expert_gate.transpose(0, 2, 1), expert_up.transpose(0, 2, 1), expert_down),
        (shared_gate.T, shared_up.T, shared_down),
        ns,
        nd,
    )
    return out.astype(BF16)[None]


def solution(mesh):
    placed = (
        P(("groups", "dp"), "seq", None),
        P(None, ("groups", "dp"), "seq", None),
        P(("groups", "dp"), "seq", None),
        P(("groups", "dp"), None),
        P(None, "dp"),
        P(),
        P(("groups", "dp"), "seq", None),
        P(("groups", "dp"), "seq", None),
        P(("seq", "dp"), None, None),
        P(("seq", "dp"), None, None),
        P(("seq", "dp"), None, None),
        P(None, "dp"),
        P(None, "dp"),
        P("dp", None),
        P(),
    )
    return jax.shard_map(
        body,
        mesh=mesh,
        in_specs=placed,
        out_specs=P(("groups", "dp"), "seq", None),
        check_vma=False,
    )
```

profile of v0, /device:TPU:528, one launch (start us, length us, event | category | flops | bytes accessed | tf_op | source)
XLA Modules:
  0.0 260.0 jit_solution(11495007844820627406)
XLA Ops:
  0.0 0.7 convert_bitcast_fusion.1
  0.7 0.7 pad_maximum_fusion.1
  1.4 0.7 pad_select_fusion.info_ref
  2.0 0.7 stack.16
  2.7 1.3 pad_maximum_fusion.vecs_ref
  4.0 254.2 %layer.1 = f32[64,2048]{1,0:T(8,128)} custom-call(s32[1,1024]{1,0:T(1,128)} %docs_ref.1, f32[8,128]{1,0:T(8,128)} %pad_select_fusion.info_ref, f32[2,2048]{1,0:T(2,128)} %pad_maximum_fusion.vecs_ref, bf16[2,64,2048]{2,1,0:T(8,128)(2,1)} %bitcast.25, bf16[64,2048]{1,0:T(8,128)(2,1)} %bitcast.26, bf16[64,2048]{1,0:T(8,128)(2,1)} %bitcast.27, ...), custom_call_target="tpu_custom_call" | custom-call | flops 5536481280 | bytes 10485760 | tf_op jit(solution)/shard_map/layer/pallas_call | solution.py:697
  258.3 1.8 convert_bitcast_fusion
where the time goes:
time: 260 us
  Pallas kernels  254 us (98%)
  other arithmetic  5.82 us (2%)
    pallas_call x1, Pallas kernels, run_layer(): pl.pallas_call(functools.partial(layer_kernel, ns, nd), out_shape=jax.Sha...  254 us

commit v1 on v0

--- a/solution.py
+++ b/solution.py
@@ -14,6 +14,7 @@
 CAP = 10
 GROUP = 2
 CORES = 2
+DIRECT = 1
 
 norm_eps = 1e-06
 MESH = pl.DeviceIdType.MESH
@@ -87,13 +88,14 @@
 
 
 def layer_kernel(
-    ns, nd, docs_ref, info_ref, vecs_ref, qk_hbm, v_hbm, resid_hbm, w_hbm, eg_hbm, eu_hbm, ed_hbm,
+    ns, nd, docs_ref, ids_ref, gates_ref, gain_ref, score_ref, qk_hbm, v_hbm, resid_hbm, w_hbm, eg_hbm, eu_hbm, ed_hbm,
     sg_hbm, su_hbm, sd_hbm, out_ref,
-    qk, v, resid, wg, wu, wd, vg, vu, vd, dcol, info, routes, qh, kh, vh, att, mixed, wall, own_sum,
+    qk, v, resid, wg, wu, wd, vg, vu, vd, vecs, dcol, spread, info, routes, qh, kh, vh, att, mixed, wall, own_sum,
     send_sum, got_sum, residual, normed, every, picks, mixes, send, own_in, pair_in, act, pair_out,
-    pair_part, own_part, back, ret, total, landed, passed,
+    pair_part, own_part, back, ret, send_pair, ret_pair, total, landed, passed,
     w_sem, local_sem, si_sem, ri_sem, so_sem, ro_sem, sd_sem, rd_sem, sp_sem, rp_sem, sw_sem, rw_sem,
-    sg_sem, rg_sem, sy_sem, ry_sem, sx_sem, rx_sem, sq_sem, rq_sem, sr_sem, rr_sem, s2_sem, r2_sem,
+    sg_sem, rg_sem, sy_sem, ry_sem, sx_sem, rx_sem, sq_sem, rq_sem, sr_sem, rr_sem, sf_sem, rf_sem, sb_sem, rb_sem,
+    s2_sem, r2_sem,
 ):
     s = lax.axis_index("seq")
     d = lax.axis_index("dp")
@@ -135,7 +137,12 @@
     lane = lax.broadcasted_iota(jnp.int32, (1, lanes), 1)
     valid = (lane >= lax.rem(d, 2) * rows) & (lane < (lax.rem(d, 2) + 1) * rows)
     expert = lax.broadcasted_iota(jnp.int32, (experts, lanes), 0).astype(F32)
-    chosen_ids = [jnp.where(valid, info_ref[k : k + 1, :], -1.0) for k in range(TOPK)]
+    spread[...] = jnp.zeros_like(spread)
+    spread[0:TOPK, 0:rows] = ids_ref[...].astype(F32)
+    spread[TOPK:, 0:rows] = gates_ref[...]
+    odd = lax.rem(d, 2).astype(F32)
+    both = spread[...] * (1.0 - odd) + pltpu.roll(spread[...], rows, 1) * odd
+    chosen_ids = [jnp.where(valid, both[k : k + 1, :], -1.0) for k in range(TOPK)]
     named = [ids == expert for ids in chosen_ids]
     earlier = lax.broadcasted_iota(jnp.int32, (lanes, lanes), 0) < lax.broadcasted_iota(
         jnp.int32, (lanes, lanes), 1
@@ -148,7 +155,11 @@
     for k in range(TOPK):
         rank = jnp.sum(jnp.where(named[k], counts, 0.0), axis=0, keepdims=True)
         info[k : k + 1, :] = jnp.where(valid, chosen_ids[k] * CAP + rank, 0.0)
-    info[TOPK:, :] = info_ref[TOPK:, :]
+    info[TOPK:, :] = both[TOPK:, :]
+    score = score_ref[...].astype(F32)
+    for i in range(width // HD):
+        vecs[0:1, i * HD : (i + 1) * HD] = gain_ref[i : i + 1, :]
+        vecs[1:2, i * HD : (i + 1) * HD] = score[i : i + 1, :]
     routes[d] = info[...]
     docs = docs_ref[...].astype(F32)
     for i in range(length // HD):
@@ -187,11 +198,15 @@
             for c, (src, dst) in enumerate(pieces(to))
         ]
 
+    def peer(j, sign):
+        chip = lax.rem(s // CORES + sign * ring_delta(j // CORES) + chips, chips)
+        return chip * CORES + lax.rem(core + j, CORES)
+
     def toward(j):
-        return lax.rem(s - ring_delta(j) + ns, ns)
+        return peer(j, -1)
 
     def origin(j):
-        return lax.rem(s + ring_delta(j) + ns, ns)
+        return peer(j, 1)
 
     @pl.loop(1, ns)
     def _(j):
@@ -357,7 +372,7 @@
     scaled = (
         stream
         * lax.rsqrt(jnp.mean(stream * stream, axis=-1, keepdims=True) + norm_eps)
-        * vecs_ref[0:1, :]
+        * vecs[0:1, :]
     ).astype(BF16)
 
     def place_of(chunk, side):
@@ -415,6 +430,20 @@
             rr_sem.at[chunk, j], device_id={"seq": origin(j)}, device_id_type=MESH,
         )
 
+    def go_pair(chunk, j):
+        return pltpu.make_async_remote_copy(
+            send_pair.at[chunk, seat(j)], pair_in.at[chunk, seat(j)], sf_sem.at[chunk, j],
+            rf_sem.at[chunk, j], device_id={"seq": toward(j)}, device_id_type=MESH,
+        )
+
+    def back_pair(chunk, j):
+        return pltpu.make_async_remote_copy(
+            pair_out.at[chunk, seat(j)], ret_pair.at[chunk, seat(j)], sb_sem.at[chunk, j],
+            rb_sem.at[chunk, j], device_id={"seq": origin(j)}, device_id_type=MESH,
+        )
+
+    near_seats = DIRECT * GROUP
+
     def columns(chunk, side):
         return pl.ds(pl.multiple_of(side * half + chunk * quarter, quarter), quarter)
 
@@ -428,11 +457,23 @@
         send[chunk, at, :] = got
         if q == 0:
             own_in[chunk, 0:slots, :] = got[0:slots]
+            near = pl.ds(0, near_seats * slots)
+            got = jnp.dot(
+                picks[near, :], every[chunk, 1 - par], preferred_element_type=F32
+            ).astype(BF16)
+            send_pair[chunk, near, :] = got
+            pair_in[chunk, 0:slots, :] = got[0:slots]
 
     def go(chunk, q):
         @pl.loop(max(1, q * batch), (q + 1) * batch)
         def _(j):
             go_copy(chunk, j).start()
+
+        if q == 0:
+
+            @pl.loop(1, near_seats)
+            def _(j):
+                go_pair(chunk, j).start()
 
     rings[0].start()
     rings[0].advance(1)
@@ -444,8 +485,9 @@
         pick(0, q)
         if q:
             go(0, q - 1)
-        rings[1].advance(q + 1)
     go(0, 3)
+    for t in range(1, nd // 2 + 1):
+        rings[1].advance(t)
     for q in range(4):
         pick(1, q)
         if q:
@@ -468,7 +510,13 @@
             def _():
                 go_copy(chunk, j).wait_recv()
 
-        swap_copy(chunk, g).start()
+            @pl.when((j > 0) & (g < DIRECT))
+            def _():
+                go_pair(chunk, j).wait_recv()
+
+        @pl.when(g >= DIRECT)
+        def _():
+            swap_copy(chunk, g).start()
 
     quads = [(chunk, side) for chunk in range(2) for side in range(2)]
     share = tokens // 4
@@ -489,7 +537,7 @@
                 gate_act += nt(a, vg[:, where])
                 up_act += nt(a, vu[:, where])
                 weight += jnp.sum(
-                    a.astype(F32) * vecs_ref[1:2, where], axis=-1, keepdims=True
+                    a.astype(F32) * vecs[1:2, where], axis=-1, keepdims=True
                 )
             hidden = (silu(gate_act) * up_act).astype(BF16)
             weight = 1.0 / (1.0 + jnp.exp(-weight))
@@ -507,13 +555,22 @@
         own_part[span_of(g), :] = jnp.dot(
             hidden, wd[:, columns(chunk, par)], preferred_element_type=F32
         )
-        part_copy(chunk, g).start()
+
+        @pl.when(g >= DIRECT)
+        def _():
+            part_copy(chunk, g).start()
 
     def join(chunk, g):
-        part_copy(chunk, g).wait_recv()
-        back[chunk, span_of(g), :] = (
-            own_part[span_of(g), :] + pair_part[chunk, span_of(g), :].astype(F32)
-        ).astype(BF16)
+        @pl.when(g >= DIRECT)
+        def _():
+            part_copy(chunk, g).wait_recv()
+            back[chunk, span_of(g), :] = (
+                own_part[span_of(g), :] + pair_part[chunk, span_of(g), :].astype(F32)
+            ).astype(BF16)
+
+        @pl.when(g < DIRECT)
+        def _():
+            back[chunk, span_of(g), :] = own_part[span_of(g), :].astype(BF16)
 
     def leave(chunk, g):
         for i in range(GROUP):
@@ -523,9 +580,14 @@
             def _():
                 back_copy(chunk, j).start()
 
+            @pl.when((j > 0) & (g < DIRECT))
+            def _():
+                back_pair(chunk, j).start()
+
             @pl.when(j == 0)
             def _():
                 ret[chunk, 0:slots, :] = back[chunk, 0:slots, :]
+                ret_pair[chunk, 0:slots, :] = pair_out[chunk, 0:slots, :]
 
     def combine(chunk, g):
         for i in range(GROUP):
@@ -535,10 +597,21 @@
             def _():
                 back_copy(chunk, j).wait_recv()
 
-        total[chunk, par] += lax.dot_general(
-            mixes[span_of(g), :], ret[chunk, span_of(g), :], (((0,), (0,)), ((), ())),
-            preferred_element_type=F32,
-        )
+            @pl.when((j > 0) & (g < DIRECT))
+            def _():
+                back_pair(chunk, j).wait_recv()
+
+        def mix(rows_in):
+            return lax.dot_general(
+                mixes[span_of(g), :], rows_in[chunk, span_of(g), :], (((0,), (0,)), ((), ())),
+                preferred_element_type=F32,
+            )
+
+        total[chunk, par] += mix(ret)
+
+        @pl.when(g < DIRECT)
+        def _():
+            total[chunk, 1 - par] += mix(ret_pair)
 
     @pl.loop(0, groups + 2)
     def _(step):
@@ -556,7 +629,10 @@
             gate_act = jnp.zeros((group_slots, wg.shape[0]), F32)
             up_act = jnp.zeros((group_slots, wg.shape[0]), F32)
             for chunk in range(2):
-                swap_copy(chunk, g).wait_recv()
+                @pl.when(g >= DIRECT)
+                def _():
+                    swap_copy(chunk, g).wait_recv()
+
                 for rows_in, side in ((own_in, par), (pair_in, 1 - par)):
                     a = rows_in[chunk, span_of(g), :]
                     gate_act += nt(a, wg[:, columns(chunk, side)])
@@ -574,9 +650,7 @@
 
     @pl.loop(0, groups)
     def _(g):
-        join(1, g)
         combine(0, g)
-        leave(1, g)
 
     last = nd // 2
 
@@ -597,18 +671,17 @@
     def target(way, t):
         return lax.rem(d + (1 - 2 * way) * t + nd, nd)
 
-    def reduce_chunk(chunk):
-        for t in range(last, 0, -1):
-            for sub in range(2):
-                for way in range(2):
-                    if not used(way, t, sub):
-                        continue
-                    term = total[chunk, :, own(target(way, t), sub), :]
-                    if used(way, t + 1, sub):
-                        hop(chunk, way, t + 1, sub).wait_recv()
-                        term = term + landed[chunk, way, t, sub].astype(F32)
-                    passed[chunk, way, t - 1, sub] = term.astype(BF16)
-                    hop(chunk, way, t, sub).start()
+    def reduce_step(chunk, t):
+        for sub in range(2):
+            for way in range(2):
+                if not used(way, t, sub):
+                    continue
+                term = total[chunk, :, own(target(way, t), sub), :]
+                if used(way, t + 1, sub):
+                    hop(chunk, way, t + 1, sub).wait_recv()
+                    term = term + landed[chunk, way, t, sub].astype(F32)
+                passed[chunk, way, t - 1, sub] = term.astype(BF16)
+                hop(chunk, way, t, sub).start()
 
     def settle(chunk):
         for sub in range(2):
@@ -624,13 +697,20 @@
                 where = pl.ds(place_of(chunk, side), quarter)
                 out_ref[at, where] = residual[at, where].astype(F32) + sums[side]
 
-    reduce_chunk(0)
+    for t in range(last, 0, -1):
+        reduce_step(0, t)
+
+        @pl.loop((last - t) * groups // last, (last - t + 1) * groups // last)
+        def _(g):
+            join(1, g)
+            leave(1, g)
 
     @pl.loop(0, groups)
     def _(g):
         combine(1, g)
 
-    reduce_chunk(1)
+    for t in range(last, 0, -1):
+        reduce_step(1, t)
     settle(0)
     settle(1)
 
@@ -647,7 +727,12 @@
             go_copy(chunk, j).wait_send()
             back_copy(chunk, j).wait_send()
 
-        @pl.loop(0, groups)
+        @pl.loop(1, near_seats)
+        def _(j):
+            go_pair(chunk, j).wait_send()
+            back_pair(chunk, j).wait_send()
+
+        @pl.loop(DIRECT, groups)
         def _(g):
             swap_copy(chunk, g).wait_send()
             part_copy(chunk, g).wait_send()
@@ -670,7 +755,7 @@
         sum_copy(index).wait_send()
 
 
-def run_layer(docs, info, vecs, qk, v, resid, out_weight, expert_weights, shared_weights, ns, nd):
+def run_layer(docs, ids, gates, gain, score, qk, v, resid, out_weight, expert_weights, shared_weights, ns, nd):
     rows, width = v.shape
     length = rows * ns
     tokens = rows * nd
@@ -678,6 +763,7 @@
     quarter = half // 2
     slots = ns * nd * CAP
     groups = ns // GROUP
+    near = DIRECT * GROUP * nd * CAP
     hidden = expert_weights[0].shape[1]
     shared_hidden = shared_weights[0].shape[0]
     dma = pltpu.SemaphoreType.DMA
@@ -694,15 +780,17 @@
     rings = dma((2, 2, nd // 2, 2))
     per_seat = dma((2, ns))
     per_group = dma((2, groups))
+    per_near = dma((2, DIRECT * GROUP))
     return pl.pallas_call(
         functools.partial(layer_kernel, ns, nd),
         out_shape=jax.ShapeDtypeStruct((rows, width), F32),
-        in_specs=[vmem] * 3 + [anyspace] * 10,
+        in_specs=[vmem] * 5 + [anyspace] * 10,
         out_specs=vmem,
         scratch_shapes=[buf(2, rows, width), buf(rows, width), buf(rows, width)]
         + [buf(hidden, width)] * 3
         + [buf(shared_hidden, width)] * 3
-        + [wide(length, HD), wide(*info.shape), wide(nd, *info.shape)]
+        + [wide(2, width), wide(length, HD)]
+        + [wide(2 * TOPK, 2 * rows), wide(2 * TOPK, 2 * rows), wide(nd, 2 * TOPK, 2 * rows)]
         + [buf(length, HD)] * 4
         + [
             buf(rows * CORES, width // CORES),
@@ -717,6 +805,7 @@
             buf(2, slots, quarter), buf(2, slots, quarter),
             wide(slots, quarter),
             buf(2, slots, quarter), buf(2, slots, quarter),
+            buf(2, near, quarter), buf(2, near, quarter),
             wide(2, 2, tokens, quarter),
             buf(2, 2, nd // 2, 2, 2, rows // 2, quarter),
             buf(2, 2, nd // 2, 2, 2, rows // 2, quarter),
@@ -724,7 +813,7 @@
             dma((ns // CORES,)), dma((nd,)), dma((nd,)), dma((nd,)), dma((nd,)),
             ring, ring, rings, rings,
             per_seat, per_seat, per_group, per_group, per_group, per_group, per_seat, per_seat,
-            rings, rings,
+            per_near, per_near, per_near, per_near, rings, rings,
         ],
         compiler_params=pltpu.CompilerParams(
             collective_id=1, has_side_effects=True, vmem_limit_bytes=67043328
@@ -733,7 +822,7 @@
             flops=12 * slots * half * hidden, bytes_accessed=8 * slots * half, transcendentals=0
         ),
         name="layer",
-    )(docs, info, vecs, qk, v, resid, out_weight, *expert_weights, *shared_weights)
+    )(docs, ids, gates, gain, score, qk, v, resid, out_weight, *expert_weights, *shared_weights)
 
 
 def body(
@@ -757,18 +846,12 @@
     nd = lax.axis_size("dp")
     tokens = resid.shape[1]
     width = resid.shape[2]
-    d = lax.axis_index("dp")
-    info = jnp.concatenate([expert_ids[0].T.astype(F32), gate_vals[0].T], axis=0)
-    blank = jnp.zeros_like(info)
-    info = jnp.where(
-        d % 2 == 0,
-        jnp.concatenate([info, blank], axis=1),
-        jnp.concatenate([blank, info], axis=1),
-    )
     out = run_layer(
         doc_ids,
-        info,
-        jnp.stack([norm_gain, shared_score.astype(F32)]),
+        expert_ids[0].T,
+        gate_vals[0].T,
+        norm_gain.reshape(-1, HD),
+        shared_score.reshape(-1, HD),
         queries_keys.reshape(2, tokens, width),
         values[0],
         resid[0],

time: 260 us -> 262 us (level)
  Pallas kernels: 254 us -> 260 us
  other arithmetic: 5.82 us -> 1.77 us
    pallas_call x1, Pallas kernels: 254 us -> 260 us  [run_layer(): pl.pallas_call(functools.partial(layer_kernel, ns, nd), out_shape=jax.Sha...]
where the time goes in v1:
time: 262 us
  Pallas kernels  260 us (99%)
    pallas_call x1, Pallas kernels, run_layer(): pl.pallas_call(functools.partial(layer_kernel, ns, nd), out_shape=jax.Sha...  260 us

profile of v1, /device:TPU:528, one launch (start us, length us, event | category | flops | bytes accessed | tf_op | source)
XLA Modules:
  0.0 262.0 jit_solution(15195201539568278266)
XLA Ops:
  0.0 260.3 %layer.1 = f32[64,2048]{1,0:T(8,128)} custom-call(s32[1,1024]{1,0:T(1,128)} %docs_ref.1, s32[4,64]{1,0:T(4,128)} %bitcast.26, f32[4,64]{1,0:T(4,128)} %bitcast.27, f32[16,128]{1,0:T(8,128)} %bitcast.24, bf16[16,128]{1,0:T(8,128)(2,1)} %bitcast.25, bf16[2,64,2048]{2,1,0:T(8,128)(2,1)} %bitcast.21, bf16[64,2048]{1,0:T(8,128)(2,1)} %bitcast.22, ...), custom_call_target="tpu_custom_call" | custom-call | flops 5536481280 | bytes 10485760 | tf_op jit(solution)/shard_map/layer/pallas_call | solution.py:784
  260.3 1.8 convert_bitcast_fusion

commit v2 on v1

--- a/solution.py
+++ b/solution.py
@@ -475,24 +475,18 @@
             def _(j):
                 go_pair(chunk, j).start()
 
-    rings[0].start()
-    rings[0].advance(1)
-    rings[0].advance(2)
-    rings[1].start()
-    rings[0].advance(3)
-    rings[0].advance(4)
-    for q in range(4):
-        pick(0, q)
-        if q:
-            go(0, q - 1)
-    go(0, 3)
-    for t in range(1, nd // 2 + 1):
-        rings[1].advance(t)
-    for q in range(4):
-        pick(1, q)
-        if q:
-            go(1, q - 1)
-    go(1, 3)
+    for ring in rings:
+        ring.start()
+    for t in range(1, nd // 2):
+        for ring in rings:
+            ring.advance(t)
+    for chunk in range(2):
+        rings[chunk].advance(nd // 2)
+        for q in range(4):
+            pick(chunk, q)
+            if q:
+                go(chunk, q - 1)
+        go(chunk, 3)
     for c in later:
         c.wait()
 
@@ -650,6 +644,8 @@
 
     @pl.loop(0, groups)
     def _(g):
+        join(1, g)
+        leave(1, g)
         combine(0, g)
 
     last = nd // 2
@@ -702,12 +698,7 @@
 
         @pl.loop((last - t) * groups // last, (last - t + 1) * groups // last)
         def _(g):
-            join(1, g)
-            leave(1, g)
-
-    @pl.loop(0, groups)
-    def _(g):
-        combine(1, g)
+            combine(1, g)
 
     for t in range(last, 0, -1):
         reduce_step(1, t)

time: 262 us -> 247 us (0.943)
  Pallas kernels: 260 us -> 244 us
    pallas_call x1, Pallas kernels: 260 us -> 244 us  [run_layer(): pl.pallas_call(functools.partial(layer_kernel, ns, nd), out_shape=jax.Sha...]
where the time goes in v2:
time: 247 us; the launch traced here: 246 us
  Pallas kernels  244 us (99%)
    pallas_call x1, Pallas kernels, run_layer(): pl.pallas_call(functools.partial(layer_kernel, ns, nd), out_shape=jax.Sha...  244 us

profile of v2, /device:TPU:528, one launch (start us, length us, event | category | flops | bytes accessed | tf_op | source)
XLA Modules:
  0.0 245.7 jit_solution(2025634072326386339)
XLA Ops:
  0.0 243.9 %layer.1 = f32[64,2048]{1,0:T(8,128)} custom-call(s32[1,1024]{1,0:T(1,128)} %docs_ref.1, s32[4,64]{1,0:T(4,128)} %bitcast.26, f32[4,64]{1,0:T(4,128)} %bitcast.27, f32[16,128]{1,0:T(8,128)} %bitcast.24, bf16[16,128]{1,0:T(8,128)(2,1)} %bitcast.25, bf16[2,64,2048]{2,1,0:T(8,128)(2,1)} %bitcast.21, bf16[64,2048]{1,0:T(8,128)(2,1)} %bitcast.22, ...), custom_call_target="tpu_custom_call" | custom-call | flops 5536481280 | bytes 10485760 | tf_op jit(solution)/shard_map/layer/pallas_call | solution.py:775
  243.9 1.8 convert_bitcast_fusion

commit v3 on v2

--- a/solution.py
+++ b/solution.py
@@ -642,11 +642,12 @@
     def _(g):
         down(1, g)
 
-    @pl.loop(0, groups)
+    @pl.loop(0, groups // 2)
     def _(g):
         join(1, g)
         leave(1, g)
-        combine(0, g)
+        combine(0, 2 * g)
+        combine(0, 2 * g + 1)
 
     last = nd // 2
 
@@ -696,9 +697,17 @@
     for t in range(last, 0, -1):
         reduce_step(0, t)
 
-        @pl.loop((last - t) * groups // last, (last - t + 1) * groups // last)
+        @pl.loop(
+            groups // 2 + (last - t) * groups // (2 * last),
+            groups // 2 + (last - t + 1) * groups // (2 * last),
+        )
         def _(g):
-            combine(1, g)
+            join(1, g)
+            leave(1, g)
+
+    @pl.loop(0, groups)
+    def _(g):
+        combine(1, g)
 
     for t in range(last, 0, -1):
         reduce_step(1, t)

time: 247 us -> 256 us (1.036)
  Pallas kernels: 244 us -> 254 us
    pallas_call x1, Pallas kernels: 244 us -> 254 us  [run_layer(): pl.pallas_call(functools.partial(layer_kernel, ns, nd), out_shape=jax.Sha...]
where the time goes in v3:
time: 256 us
  Pallas kernels  254 us (99%)
    pallas_call x1, Pallas kernels, run_layer(): pl.pallas_call(functools.partial(layer_kernel, ns, nd), out_shape=jax.Sha...  254 us

profile of v3, /device:TPU:528, one launch (start us, length us, event | category | flops | bytes accessed | tf_op | source)
XLA Modules:
  0.0 255.8 jit_solution(4258471965310521114)
XLA Ops:
  0.0 254.1 %layer.1 = f32[64,2048]{1,0:T(8,128)} custom-call(s32[1,1024]{1,0:T(1,128)} %docs_ref.1, s32[4,64]{1,0:T(4,128)} %bitcast.26, f32[4,64]{1,0:T(4,128)} %bitcast.27, f32[16,128]{1,0:T(8,128)} %bitcast.24, bf16[16,128]{1,0:T(8,128)(2,1)} %bitcast.25, bf16[2,64,2048]{2,1,0:T(8,128)(2,1)} %bitcast.21, bf16[64,2048]{1,0:T(8,128)(2,1)} %bitcast.22, ...), custom_call_target="tpu_custom_call" | custom-call | flops 5536481280 | bytes 10485760 | tf_op jit(solution)/shard_map/layer/pallas_call | solution.py:784
  254.1 1.8 convert_bitcast_fusion

commit v4 on v2

--- a/solution.py
+++ b/solution.py
@@ -14,7 +14,7 @@
 CAP = 10
 GROUP = 2
 CORES = 2
-DIRECT = 1
+DIRECT = (1, 2)
 
 norm_eps = 1e-06
 MESH = pl.DeviceIdType.MESH
@@ -442,7 +442,7 @@
             rb_sem.at[chunk, j], device_id={"seq": origin(j)}, device_id_type=MESH,
         )
 
-    near_seats = DIRECT * GROUP
+    near_seats = [count * GROUP for count in DIRECT]
 
     def columns(chunk, side):
         return pl.ds(pl.multiple_of(side * half + chunk * quarter, quarter), quarter)
@@ -457,7 +457,7 @@
         send[chunk, at, :] = got
         if q == 0:
             own_in[chunk, 0:slots, :] = got[0:slots]
-            near = pl.ds(0, near_seats * slots)
+            near = pl.ds(0, near_seats[chunk] * slots)
             got = jnp.dot(
                 picks[near, :], every[chunk, 1 - par], preferred_element_type=F32
             ).astype(BF16)
@@ -471,7 +471,7 @@
 
         if q == 0:
 
-            @pl.loop(1, near_seats)
+            @pl.loop(1, near_seats[chunk])
             def _(j):
                 go_pair(chunk, j).start()
 
@@ -504,11 +504,11 @@
             def _():
                 go_copy(chunk, j).wait_recv()
 
-            @pl.when((j > 0) & (g < DIRECT))
+            @pl.when((j > 0) & (g < DIRECT[chunk]))
             def _():
                 go_pair(chunk, j).wait_recv()
 
-        @pl.when(g >= DIRECT)
+        @pl.when(g >= DIRECT[chunk])
         def _():
             swap_copy(chunk, g).start()
 
@@ -550,19 +550,19 @@
             hidden, wd[:, columns(chunk, par)], preferred_element_type=F32
         )
 
-        @pl.when(g >= DIRECT)
+        @pl.when(g >= DIRECT[chunk])
         def _():
             part_copy(chunk, g).start()
 
     def join(chunk, g):
-        @pl.when(g >= DIRECT)
+        @pl.when(g >= DIRECT[chunk])
         def _():
             part_copy(chunk, g).wait_recv()
             back[chunk, span_of(g), :] = (
                 own_part[span_of(g), :] + pair_part[chunk, span_of(g), :].astype(F32)
             ).astype(BF16)
 
-        @pl.when(g < DIRECT)
+        @pl.when(g < DIRECT[chunk])
         def _():
             back[chunk, span_of(g), :] = own_part[span_of(g), :].astype(BF16)
 
@@ -574,7 +574,7 @@
             def _():
                 back_copy(chunk, j).start()
 
-            @pl.when((j > 0) & (g < DIRECT))
+            @pl.when((j > 0) & (g < DIRECT[chunk]))
             def _():
                 back_pair(chunk, j).start()
 
@@ -591,7 +591,7 @@
             def _():
                 back_copy(chunk, j).wait_recv()
 
-            @pl.when((j > 0) & (g < DIRECT))
+            @pl.when((j > 0) & (g < DIRECT[chunk]))
             def _():
                 back_pair(chunk, j).wait_recv()
 
@@ -603,7 +603,7 @@
 
         total[chunk, par] += mix(ret)
 
-        @pl.when(g < DIRECT)
+        @pl.when(g < DIRECT[chunk])
         def _():
             total[chunk, 1 - par] += mix(ret_pair)
 
@@ -623,7 +623,7 @@
             gate_act = jnp.zeros((group_slots, wg.shape[0]), F32)
             up_act = jnp.zeros((group_slots, wg.shape[0]), F32)
             for chunk in range(2):
-                @pl.when(g >= DIRECT)
+                @pl.when(g >= DIRECT[chunk])
                 def _():
                     swap_copy(chunk, g).wait_recv()
 
@@ -693,15 +693,17 @@
                 where = pl.ds(place_of(chunk, side), quarter)
                 out_ref[at, where] = residual[at, where].astype(F32) + sums[side]
 
-    for t in range(last, 0, -1):
-        reduce_step(0, t)
-
-        @pl.loop((last - t) * groups // last, (last - t + 1) * groups // last)
-        def _(g):
-            combine(1, g)
+    reduce_step(0, last)
+    reduce_step(0, last - 1)
+
+    @pl.loop(0, groups)
+    def _(g):
+        combine(1, g)
 
     for t in range(last, 0, -1):
         reduce_step(1, t)
+        if t > 2:
+            reduce_step(0, t - 2)
     settle(0)
     settle(1)
 
@@ -718,12 +720,12 @@
             go_copy(chunk, j).wait_send()
             back_copy(chunk, j).wait_send()
 
-        @pl.loop(1, near_seats)
+        @pl.loop(1, near_seats[chunk])
         def _(j):
             go_pair(chunk, j).wait_send()
             back_pair(chunk, j).wait_send()
 
-        @pl.loop(DIRECT, groups)
+        @pl.loop(DIRECT[chunk], groups)
         def _(g):
             swap_copy(chunk, g).wait_send()
             part_copy(chunk, g).wait_send()
@@ -754,7 +756,7 @@
     quarter = half // 2
     slots = ns * nd * CAP
     groups = ns // GROUP
-    near = DIRECT * GROUP * nd * CAP
+    near = max(DIRECT) * GROUP * nd * CAP
     hidden = expert_weights[0].shape[1]
     shared_hidden = shared_weights[0].shape[0]
     dma = pltpu.SemaphoreType.DMA
@@ -771,7 +773,7 @@
     rings = dma((2, 2, nd // 2, 2))
     per_seat = dma((2, ns))
     per_group = dma((2, groups))
-    per_near = dma((2, DIRECT * GROUP))
+    per_near = dma((2, max(DIRECT) * GROUP))
     return pl.pallas_call(
         functools.partial(layer_kernel, ns, nd),
         out_shape=jax.ShapeDtypeStruct((rows, width), F32),

time: 247 us -> 251 us (1.016)
  Pallas kernels: 244 us -> 247 us
    pallas_call x1, Pallas kernels: 244 us -> 247 us  [run_layer(): pl.pallas_call(functools.partial(layer_kernel, ns, nd), out_shape=jax.Sha...]
where the time goes in v4:
time: 251 us; the launch traced here: 249 us
  Pallas kernels  247 us (98%)
    pallas_call x1, Pallas kernels, run_layer(): pl.pallas_call(functools.partial(layer_kernel, ns, nd), out_shape=jax.Sha...  247 us

profile of v4, /device:TPU:528, one launch (start us, length us, event | category | flops | bytes accessed | tf_op | source)
XLA Modules:
  0.0 249.1 jit_solution(6123749527484986526)
XLA Ops:
  0.0 247.3 %layer.1 = f32[64,2048]{1,0:T(8,128)} custom-call(s32[1,1024]{1,0:T(1,128)} %docs_ref.1, s32[4,64]{1,0:T(4,128)} %bitcast.26, f32[4,64]{1,0:T(4,128)} %bitcast.27, f32[16,128]{1,0:T(8,128)} %bitcast.24, bf16[16,128]{1,0:T(8,128)(2,1)} %bitcast.25, bf16[2,64,2048]{2,1,0:T(8,128)(2,1)} %bitcast.21, bf16[64,2048]{1,0:T(8,128)(2,1)} %bitcast.22, ...), custom_call_target="tpu_custom_call" | custom-call | flops 5536481280 | bytes 10485760 | tf_op jit(solution)/shard_map/layer/pallas_call | solution.py:777
  247.3 1.8 convert_bitcast_fusion

commit v5 on v2

--- a/solution.py
+++ b/solution.py
@@ -640,12 +640,12 @@
 
     @pl.loop(0, groups)
     def _(g):
-        down(1, g)
+        down(1, groups - 1 - g)
 
     @pl.loop(0, groups)
     def _(g):
-        join(1, g)
-        leave(1, g)
+        join(1, groups - 1 - g)
+        leave(1, groups - 1 - g)
         combine(0, g)
 
     last = nd // 2
@@ -698,7 +698,7 @@
 
         @pl.loop((last - t) * groups // last, (last - t + 1) * groups // last)
         def _(g):
-            combine(1, g)
+            combine(1, groups - 1 - g)
 
     for t in range(last, 0, -1):
         reduce_step(1, t)

time: 247 us -> 250 us (1.012)
  no operation moved by 1% of the time
where the time goes in v5:
time: 250 us; the launch traced here: 248 us
  Pallas kernels  246 us (98%)
    pallas_call x1, Pallas kernels, run_layer(): pl.pallas_call(functools.partial(layer_kernel, ns, nd), out_shape=jax.Sha...  246 us

profile of v5, /device:TPU:528, one launch (start us, length us, event | category | flops | bytes accessed | tf_op | source)
XLA Modules:
  0.0 247.9 jit_solution(14349056872338666207)
XLA Ops:
  0.0 246.2 %layer.1 = f32[64,2048]{1,0:T(8,128)} custom-call(s32[1,1024]{1,0:T(1,128)} %docs_ref.1, s32[4,64]{1,0:T(4,128)} %bitcast.26, f32[4,64]{1,0:T(4,128)} %bitcast.27, f32[16,128]{1,0:T(8,128)} %bitcast.24, bf16[16,128]{1,0:T(8,128)(2,1)} %bitcast.25, bf16[2,64,2048]{2,1,0:T(8,128)(2,1)} %bitcast.21, bf16[64,2048]{1,0:T(8,128)(2,1)} %bitcast.22, ...), custom_call_target="tpu_custom_call" | custom-call | flops 5536481280 | bytes 10485760 | tf_op jit(solution)/shard_map/layer/pallas_call | solution.py:775
  246.2 1.8 convert_bitcast_fusion
